TPU v7x, 32 devices: a whole 2x2x4 slice. The times are simulated.
32 devices in a mesh: seq: 16 (over z, y, x), tensor: 2 (over core).
Axes of the slice: x: 2, y: 2, z: 4, core: 2. Of those that a mesh axis runs over, the one named last changes fastest.
Arguments:
- hidden: bfloat16 [2, 4096, 8192], P(None, 'seq', 'tensor'), may hold values from -160 to 160
- norm_gain: bfloat16 [8192], P('tensor'), may hold values from 0.25 to 1.75
- value_weight: bfloat16 [8192], P('tensor'), may hold values from -0.0625 to 0.0625
- rewards: float32 [2, 4096], P(None, 'seq'), may hold values from -6 to 6
- done_flags: int32 [2, 4096], P(None, 'seq'), may hold values 0 or 1
- valid_mask: int32 [2, 4096], P('tensor', 'seq'), may hold values 0 or 1
- new_logprob: float32 [2, 4096], P('tensor', 'seq'), may hold values from -1 to 1
- old_logprob: float32 [2, 4096], P('tensor', 'seq'), may hold values from -1 to 1
- discount: float32 [2], replicated, may hold values from 0.9 to 1
- trace_decay: float32 [2], replicated, may hold values from 0.9 to 1
- bootstrap: float32 [2], replicated, may hold values from -5 to 5
Outputs:
- values: float32 [2, 4096], P('tensor', 'seq')
- white_adv: float32 [2, 4096], P('tensor', 'seq')
- token_loss: float32 [2, 4096], P('tensor', 'seq')
- policy_loss: float32 [], replicated
All inputs are finite; a program needn't handle non-finite values. No bound on the sum of `done_flags` or of `valid_mask` on one device may be relied on, other than what follows from the above.
Results may differ from a plain program's by a relative error of at most 0.00035.
Values sent between devices are 32-bit elements; how exact they have to be, the bound alone decides.
A program may use at most 64 MiB of HBM per device.

v0:
```python
import functools

import jax
import jax.numpy as jnp
from jax import lax
from jax.experimental import pallas as pl
from jax.experimental.pallas import tpu as pltpu
from jax.sharding import PartitionSpec as P

EPS_NORM = 1e-06
EPS_WHITE = 1e-08
CLIP = 0.2
LANES = 128
BLOCK = 32
UNROLLED = 64
IN_FLIGHT = 4


def lane_sums(parts):
    total = 0.0
    for _ in range(3):
        piece = parts.astype(jnp.bfloat16)
        parts = parts - piece.astype(jnp.float32)
        total = total + lax.dot_general(
            jnp.ones((8, LANES), jnp.bfloat16),
            piece,
            (((1,), (1,)), ((), ())),
            preferred_element_type=jnp.float32,
        )
    return total


def kernel(
    seq_count,
    tensor_count,
    width,
    chunk,
    hidden_hbm,
    gain_hbm,
    weight_hbm,
    rewards_hbm,
    flags_hbm,
    mask_hbm,
    new_hbm,
    old_hbm,
    discount_hbm,
    trace_hbm,
    boot_hbm,
    values_ref,
    white_ref,
    token_ref,
    loss_ref,
    hid,
    gain,
    wgt,
    rew,
    flg,
    msk,
    newp,
    oldp,
    disc,
    trc,
    boot,
    scaled,
    parts,
    part_send,
    part_recv,
    early,
    late,
    carry,
    slope,
    hid_sem,
    in_sem,
    part_send_sem,
    part_recv_sem,
    early_send_sem,
    early_recv_sem,
    late_send_sem,
    late_recv_sem,
):
    seqs_all, length, local_width = hid.shape
    own_rows = seqs_all // tensor_count
    devices = seq_count * tensor_count
    chunks = length // chunk
    me_seq = lax.axis_index("seq")
    me_ten = lax.axis_index("tensor")
    first_row = me_ten * own_rows
    my_slot = me_ten * seq_count + me_seq

    small = [
        (gain_hbm, gain),
        (weight_hbm, wgt),
        (rewards_hbm, rew),
        (flags_hbm, flg),
        (mask_hbm, msk),
        (new_hbm, newp),
        (old_hbm, oldp),
        (discount_hbm, disc),
        (trace_hbm, trc),
        (boot_hbm, boot),
    ]
    small_copies = [
        pltpu.make_async_copy(src, dst, in_sem.at[i]) for i, (src, dst) in enumerate(small)
    ]
    for copy in small_copies:
        copy.start()

    def hid_copy(i, c):
        row = lax.rem(first_row + own_rows + i, seqs_all)
        rows = pl.ds(c * chunk, chunk)
        return pltpu.make_async_copy(
            hidden_hbm.at[row, rows, :], hid.at[i, rows, :], hid_sem.at[i * chunks + c]
        )

    for g in range(min(IN_FLIGHT, seqs_all * chunks)):
        hid_copy(g // chunks, g % chunks).start()

    barrier = pltpu.get_barrier_semaphore()

    def peer(k):
        slot = lax.rem(my_slot + k, devices)
        return (lax.rem(slot, seq_count), lax.div(slot, seq_count))

    def each_peer(act):
        if devices <= UNROLLED:
            for k in range(1, devices):
                act(k, 0)
        else:
            lax.fori_loop(1, devices, act, 0)

    def greet(k, _):
        pl.semaphore_signal(
            barrier, inc=1, device_id=peer(k), device_id_type=pl.DeviceIdType.MESH
        )
        return 0

    each_peer(greet)

    for copy in small_copies:
        copy.wait()

    for j in range(local_width // LANES):
        cols = pl.ds(j * LANES, LANES)
        row = gain[cols].astype(jnp.float32) * wgt[cols].astype(jnp.float32)
        scaled[:, cols] = jnp.broadcast_to(row.reshape(1, LANES), (8, LANES))

    lane = lax.broadcasted_iota(jnp.int32, (8, length), 1)
    steps = []
    step = 1
    while step < length:
        steps.append(step)
        step *= 4
    ahead = lambda x, d: pltpu.roll(x, (length - d) % length, 1)
    rows_info = []
    tasks = []

    def scan_task(info, d):
        def run():
            one = info["level"]
            two = one * ahead(one, d)
            info["levels"] += [(d, one), (2 * d, two), (3 * d, one * ahead(two, d))]
            info["level"] = two * ahead(two, 2 * d)

        return run

    def coef_of(last_done, row):
        shape = last_done.shape[:-1] + (length,)
        at = lax.broadcasted_iota(jnp.int32, shape, len(shape) - 1).astype(jnp.float32)
        discount = jnp.full(shape, disc[row], jnp.float32)
        decay = discount * jnp.full(shape, trc[row], jnp.float32)
        power = jnp.exp((length - 1.0 - at) * jnp.log(decay))
        return jnp.where(at > last_done[..., 0:1], discount * power, 0.0)

    for r in range(own_rows):
        discount = jnp.full((8, length), disc[first_row + r], jnp.float32)
        trace = jnp.full((8, length), trc[first_row + r], jnp.float32)
        flags = jnp.broadcast_to(flg[pl.ds(first_row + r, 1), :], (8, length))
        alive = 1.0 - flags.astype(jnp.float32)
        ratio = jnp.exp(newp[r : r + 1, :] - oldp[r : r + 1, :])
        weight = msk[r : r + 1, :].astype(jnp.float32)
        reward = jnp.broadcast_to(rew[pl.ds(first_row + r, 1), :], (8, length))
        last_done = jnp.max(
            jnp.where(flags > 0, lane, -1).astype(jnp.float32)[0:1, :], axis=1, keepdims=True
        )
        info = dict(
            trace=trace,
            level=jnp.where(lane < length - 1, discount * trace * alive, 0.0),
            levels=[],
            ratio=ratio,
            weight=weight,
            reward=reward,
            following=jnp.where(lane < length - 1, discount * alive, 0.0),
        )
        rows_info.append(info)
        tasks += [scan_task(info, d) for d in steps]
        early[my_slot, r : r + 1, 0:length] = ratio
        early[my_slot, r : r + 1, length : 2 * length] = weight
        early[my_slot, r : r + 1, 2 * length : 2 * length + LANES] = jnp.broadcast_to(
            last_done, (1, LANES)
        )
    all_chunks = seqs_all * chunks
    task_count = len(tasks)

    def row_sums(i):
        start, squares_rows, products_rows = 0, [], []
        for c in range(chunks):
            g = i * chunks + c
            hid_copy(i, c).wait()
            if g + IN_FLIGHT < all_chunks:
                hid_copy((g + IN_FLIGHT) // chunks, (g + IN_FLIGHT) % chunks).start()
            for task in tasks[g * task_count // all_chunks : (g + 1) * task_count // all_chunks]:
                task()
            for b in range(chunk // BLOCK):
                rows = pl.ds(c * chunk + b * BLOCK, BLOCK)
                squares = jnp.zeros((BLOCK // 8, 8, LANES), jnp.float32)
                products = jnp.zeros((BLOCK // 8, 8, LANES), jnp.float32)
                for j in range(local_width // LANES):
                    cols = pl.ds(j * LANES, LANES)
                    x = hid[i, rows, cols].astype(jnp.float32).reshape(BLOCK // 8, 8, LANES)
                    squares = squares + x * x
                    products = products + x * scaled[:, cols][None]
                parts[0, rows, :] = squares.reshape(BLOCK, LANES)
                parts[1, rows, :] = products.reshape(BLOCK, LANES)
            done = (c + 1) * chunk
            if done % LANES == 0 or done == length:
                rows = pl.ds(start, done - start)
                squares_rows.append(lane_sums(parts[0, rows, :]))
                products_rows.append(lane_sums(parts[1, rows, :]))
                start = done
        return jnp.concatenate(squares_rows, axis=1), jnp.concatenate(products_rows, axis=1)

    for k in range(1, tensor_count):
        for r in range(own_rows):
            squares, products = row_sums((k - 1) * own_rows + r)
            part_send[k - 1, 2 * r : 2 * r + 1, :] = squares[0:1, :]
            part_send[k - 1, 2 * r + 1 : 2 * r + 2, :] = products[0:1, :]

    pl.semaphore_wait(barrier, devices - 1)

    part_copies = []
    for k in range(1, tensor_count):
        copy = pltpu.make_async_remote_copy(
            src_ref=part_send.at[k - 1],
            dst_ref=part_recv.at[k - 1],
            send_sem=part_send_sem.at[k - 1],
            recv_sem=part_recv_sem.at[k - 1],
            device_id=(me_seq, lax.rem(me_ten + k, tensor_count)),
            device_id_type=pl.DeviceIdType.MESH,
        )
        copy.start()
        part_copies.append(copy)

    def send_all(buffer, send_sem, recv_sem):
        def send(k, _):
            pltpu.make_async_remote_copy(
                src_ref=buffer.at[my_slot],
                dst_ref=buffer.at[my_slot],
                send_sem=send_sem,
                recv_sem=recv_sem,
                device_id=peer(k),
                device_id_type=pl.DeviceIdType.MESH,
            ).start()
            return 0

        each_peer(send)

    def all_blocks(buffer, sem):
        view = buffer.at[pl.ds(0, devices - 1)]
        return pltpu.make_async_copy(view, view, sem)

    send_all(early, early_send_sem, early_recv_sem)

    own = [row_sums((tensor_count - 1) * own_rows + r) for r in range(own_rows)]
    for copy in part_copies:
        copy.wait()

    for r in range(own_rows):
        info = rows_info[r]
        trace, levels, reward, following = (
            info[name] for name in ("trace", "levels", "reward", "following")
        )
        squares, products = own[r]
        for k in range(1, tensor_count):
            squares = squares + part_recv[k - 1, 2 * r : 2 * r + 1, :]
            products = products + part_recv[k - 1, 2 * r + 1 : 2 * r + 2, :]
        values = products * lax.rsqrt(squares / width + EPS_NORM)
        values_ref[r : r + 1, :] = values[0:1, :]
        adv = reward + following * ahead(values, 1) - values
        for n in range(0, len(levels), 3):
            adv = adv + sum(level * ahead(adv, d) for d, level in levels[n : n + 3] if d < length)
        late[my_slot, r : r + 1, 0:length] = adv[0:1, :]
        late[my_slot, r : r + 1, length : length + LANES] = jnp.broadcast_to(
            values[0:1, 0:1] + trace[0:1, 0:1] * adv[0:1, 0:1], (1, LANES)
        )

    send_all(late, late_send_sem, late_recv_sem)

    all_blocks(early, early_recv_sem).wait()
    count = jnp.zeros((seq_count, length), jnp.float32)
    for t in range(tensor_count):
        for r in range(own_rows):
            count = count + early[pl.ds(t * seq_count, seq_count), r, length : 2 * length]
    total = lambda x: jnp.sum(jnp.sum(x, axis=0, keepdims=True), axis=1, keepdims=True)
    count = total(count)
    coefs = []
    for t in range(tensor_count):
        for r in range(own_rows):
            row = t * own_rows + r
            slots = pl.ds(t * seq_count, seq_count)
            coef = coef_of(early[slots, r, 2 * length : 2 * length + LANES], row)
            coefs.append(coef)
            slope[slots, r, :] = jnp.broadcast_to(trc[row] * coef[:, 0:1], (seq_count, LANES))
    all_blocks(late, late_recv_sem).wait()

    advs = []
    for t in range(tensor_count):
        for r in range(own_rows):
            entering = jnp.full((1, LANES), boot[t * own_rows + r], jnp.float32)
            for n in range(seq_count - 1, -1, -1):
                slot = t * seq_count + n
                carry[slot, r : r + 1, :] = entering
                if n:
                    offset = late[slot, r : r + 1, length : length + LANES]
                    entering = offset + slope[slot, r : r + 1, :] * entering
    sums = jnp.zeros((seq_count, length), jnp.float32)
    for t in range(tensor_count):
        for r in range(own_rows):
            slots = pl.ds(t * seq_count, seq_count)
            entering = jnp.concatenate([carry[slots, r, :]] * (length // LANES), axis=1)
            adv = late[slots, r, 0:length] + coefs[t * own_rows + r] * entering
            advs.append(adv)
            sums = sums + early[slots, r, length : 2 * length] * adv
    mean = total(sums) / count
    sums = jnp.zeros((seq_count, length), jnp.float32)
    for t in range(tensor_count):
        for r in range(own_rows):
            slots = pl.ds(t * seq_count, seq_count)
            centred = advs[t * own_rows + r] - mean
            advs[t * own_rows + r] = centred
            sums = sums + early[slots, r, length : 2 * length] * centred * centred
    scale = lax.rsqrt(total(sums) / count + EPS_WHITE)

    def token_loss(ratio, weight, white):
        clipped = jnp.clip(ratio, 1.0 - CLIP, 1.0 + CLIP)
        return -weight * jnp.minimum(ratio * white, clipped * white)

    for r in range(own_rows):
        ratio, weight = rows_info[r]["ratio"], rows_info[r]["weight"]
        coef = coef_of(early[my_slot, r : r + 1, 2 * length : 2 * length + LANES], first_row + r)
        entering = carry[my_slot, r : r + 1, :]
        entering = jnp.concatenate([entering] * (length // LANES), axis=1)
        adv = late[my_slot, r : r + 1, 0:length] + coef * entering
        white = (adv - mean) * scale
        white_ref[r : r + 1, :] = white
        token_ref[r : r + 1, :] = token_loss(ratio, weight, white)

    sums = jnp.zeros((seq_count, length), jnp.float32)
    for t in range(tensor_count):
        for r in range(own_rows):
            slots = pl.ds(t * seq_count, seq_count)
            sums = sums + token_loss(
                early[slots, r, 0:length],
                early[slots, r, length : 2 * length],
                advs[t * own_rows + r] * scale,
            )
    loss_ref[...] = jnp.broadcast_to(total(sums) / count, (1, LANES))

    all_blocks(early, early_send_sem).wait()
    all_blocks(late, late_send_sem).wait()


def write_out(*refs):
    half = len(refs) // 2
    for src, dst in zip(refs[:half], refs[half:]):
        dst[...] = src[:, : dst.shape[1]]


def shards(seq_count, tensor_count, *args):
    seqs_all, length, local_width = args[0].shape
    own_rows = seqs_all // tensor_count
    devices = seq_count * tensor_count
    chunk = min(length, 64)
    f32 = jnp.float32
    row = jax.ShapeDtypeStruct((own_rows, length), f32)
    dma = pltpu.SemaphoreType.DMA
    shapes = [row, row, row, jax.ShapeDtypeStruct((1, 1), f32)]
    outs = pl.pallas_call(
        functools.partial(kernel, seq_count, tensor_count, local_width * tensor_count, chunk),
        out_shape=[row, row, row, jax.ShapeDtypeStruct((1, LANES), f32)],
        in_specs=[pl.BlockSpec(memory_space=pltpu.HBM)] * 11,
        out_specs=[pl.BlockSpec(memory_space=pltpu.VMEM)] * 4,
        scratch_shapes=[
            pltpu.VMEM((seqs_all, length, local_width), jnp.bfloat16),
            pltpu.VMEM((local_width,), jnp.bfloat16),
            pltpu.VMEM((local_width,), jnp.bfloat16),
            pltpu.VMEM((seqs_all, length), f32),
            pltpu.VMEM((seqs_all, length), jnp.int32),
            pltpu.VMEM((own_rows, length), jnp.int32),
            pltpu.VMEM((own_rows, length), f32),
            pltpu.VMEM((own_rows, length), f32),
            pltpu.SMEM((seqs_all,), f32),
            pltpu.SMEM((seqs_all,), f32),
            pltpu.SMEM((seqs_all,), f32),
            pltpu.VMEM((8, local_width), f32),
            pltpu.VMEM((2, length, LANES), f32),
            pltpu.VMEM((max(tensor_count - 1, 1), 2 * own_rows, length), f32),
            pltpu.VMEM((max(tensor_count - 1, 1), 2 * own_rows, length), f32),
            pltpu.VMEM((devices, own_rows, 2 * length + LANES), f32),
            pltpu.VMEM((devices, own_rows, length + LANES), f32),
            pltpu.VMEM((devices, own_rows, LANES), f32),
            pltpu.VMEM((devices, own_rows, LANES), f32),
            dma((seqs_all * (length // chunk),)),
            dma((10,)),
            dma((max(tensor_count - 1, 1),)),
            dma((max(tensor_count - 1, 1),)),
            dma,
            dma,
            dma,
            dma,
        ],
        compiler_params=pltpu.CompilerParams(
            collective_id=0, has_side_effects=True, vmem_limit_bytes=24 << 20
        ),
    )(*[pltpu.with_memory_space_constraint(x, pltpu.HBM) for x in args])
    outs = pl.pallas_call(
        write_out,
        out_shape=shapes,
        in_specs=[pl.BlockSpec(memory_space=pltpu.VMEM)] * 4,
        out_specs=[pl.BlockSpec(memory_space=pltpu.VMEM)] * 4,
        compiler_params=pltpu.CompilerParams(vmem_limit_bytes=1 << 20),
    )(*outs)
    return (outs[0], outs[1], outs[2], outs[3].reshape(()))


def solution(mesh):
    in_specs = (
        P(None, "seq", "tensor"),
        P("tensor"),
        P("tensor"),
        P(None, "seq"),
        P(None, "seq"),
        P("tensor", "seq"),
        P("tensor", "seq"),
        P("tensor", "seq"),
        P(),
        P(),
        P(),
    )
    out_specs = (P("tensor", "seq"), P("tensor", "seq"), P("tensor", "seq"), P())
    body = functools.partial(shards, mesh.shape["seq"], mesh.shape["tensor"])
    return jax.shard_map(body, mesh=mesh, in_specs=in_specs, out_specs=out_specs, check_vma=False)
```

profile of v0, /device:TPU:0, one launch (start us, length us, event | category | flops | bytes accessed | tf_op | source)
XLA Modules:
  0.0 14.4 jit_solution(5140261610321761891)
XLA Ops:
  0.6 13.1 %shard_map.138 = (f32[1,256]{1,0:T(1,128)S(1)}, f32[1,256]{1,0:T(1,128)S(1)}, f32[1,256]{1,0:T(1,128)S(1)}, f32[1,128]{1,0:T(1,128)S(1)}) custom-call(bf16[2,256,4096]{2,1,0:T(8,128)(2,1)} %hidden_hbm.1, bf16[4096]{0:T(1024)(128)(2,1)} %gain_hbm.1, bf16[4096]{0:T(1024)(128)(2,1)} %weight_hbm.1, f32[2,256]{1,0:T(2,128)} %rewards_hbm.1, s32[2,256]{1,0:T(2,128)} %flags_hbm.1, ...), custom_call_target="tpu_custom_call" | custom-call | tf_op jit(solution)/shard_map/pallas_call | solution.py:387
  13.8 0.6 %shard_map.139 = (f32[1,256]{1,0:T(1,128)}, f32[1,256]{1,0:T(1,128)}, f32[1,256]{1,0:T(1,128)}, f32[1,1]{1,0:T(1,128)}) custom-call(f32[1,256]{1,0:T(1,128)S(1)} %get-tuple-element.12.refs_0_, f32[1,256]{1,0:T(1,128)S(1)} %get-tuple-element.13.refs_1_, f32[1,256]{1,0:T(1,128)S(1)} %get-tuple-element.14.refs_2_, f32[1,128]{1,0:T(1,128)S(1)} %get-tuple-element.15.refs_3_), custom_call_target="tpu_custom_call" | custom-call | tf_op jit(solution)/shard_map/pallas_call | solution.py:425
where the time goes:
time: 14.6 us; the launch traced here: 14.4 us
  Pallas kernels  13.7 us (94%)
  between operations  0.64 us (4%)
    pallas_call x1, Pallas kernels, shards(): pl.pallas_call(functools.partial(kernel, seq_count, tensor_count, local_w...  13.1 us
    pallas_call x1, Pallas kernels, shards(): pl.pallas_call(write_out, out_shape=shapes, in_specs=[pl.BlockSpec(memory...  0.58 us

commit v1 on v0

v1 whole, which is shorter than its diff:
```python
import functools

import jax
import jax.numpy as jnp
from jax import lax
from jax.experimental import pallas as pl
from jax.experimental.pallas import tpu as pltpu
from jax.sharding import PartitionSpec as P

EPS_NORM = 1e-06
EPS_WHITE = 1e-08
CLIP = 0.2
LANES = 128
BLOCK = 32
UNROLLED = 64
AHEAD_ROWS = 2


def split(parts, count):
    pieces = []
    for _ in range(count):
        pieces.append(parts.astype(jnp.bfloat16))
        parts = parts - pieces[-1].astype(jnp.float32)
    return pieces


def lane_sums(ones, pieces):
    return lax.dot_general(
        ones,
        jnp.concatenate(pieces, axis=1),
        (((1,), (1,)), ((), ())),
        preferred_element_type=jnp.float32,
    )


def kernel(
    seq_count,
    tensor_count,
    width,
    chunk,
    hidden_hbm,
    gain_hbm,
    weight_hbm,
    rewards_hbm,
    flags_hbm,
    mask_hbm,
    new_hbm,
    old_hbm,
    discount_hbm,
    trace_hbm,
    boot_hbm,
    values_ref,
    white_ref,
    token_ref,
    loss_ref,
    hid,
    gain,
    wgt,
    rew,
    flg,
    msk,
    newp,
    oldp,
    disc,
    trc,
    boot,
    ruler,
    scaled,
    parts,
    reach,
    part_send,
    part_recv,
    board,
    carry,
    slope,
    hid_sem,
    near_sem,
    far_sem,
    scalar_sem,
    part_send_sem,
    part_recv_sem,
    send_sem,
    early_recv_sem,
    late_recv_sem,
):
    seqs_all, length, local_width = hid.shape
    own_rows = seqs_all // tensor_count
    devices = seq_count * tensor_count
    chunks = length // chunk
    me_seq = lax.axis_index("seq")
    me_ten = lax.axis_index("tensor")
    first_row = me_ten * own_rows
    my_slot = me_ten * seq_count + me_seq
    early_lanes = pl.ds(0, 2 * length + LANES)
    late_lanes = pl.ds(2 * length + LANES, length + LANES)
    weight_lanes = pl.ds(length, length)
    done_lanes = pl.ds(2 * length, LANES)
    adv_lanes = pl.ds(2 * length + LANES, length)
    offset_lanes = pl.ds(3 * length + LANES, LANES)

    near = [(gain_hbm, gain), (weight_hbm, wgt), (flags_hbm, flg)]
    scalars = [(discount_hbm, disc), (trace_hbm, trc), (boot_hbm, boot)]
    far = [(rewards_hbm, rew), (mask_hbm, msk), (new_hbm, newp), (old_hbm, oldp)]

    def wait_group(group, sem):
        size = sum(dst.size * dst.dtype.itemsize for _, dst in group)
        view = ruler.at[pl.ds(0, size // (4 * LANES))]
        pltpu.make_async_copy(view, view, sem).wait()

    ahead_rows = hid_sem.shape[0] // chunks

    def hid_copy(i, c):
        row = lax.rem(first_row + own_rows + i, seqs_all)
        rows = pl.ds(c * chunk, chunk)
        sem = hid_sem.at[i % ahead_rows * chunks + c]
        return pltpu.make_async_copy(hidden_hbm.at[row, rows, :], hid.at[i, rows, :], sem)

    for src, dst in near:
        pltpu.make_async_copy(src, dst, near_sem).start()
    for src, dst in far:
        pltpu.make_async_copy(src, dst, far_sem).start()
    scalar_copies = [
        pltpu.make_async_copy(src, dst, scalar_sem.at[i]) for i, (src, dst) in enumerate(scalars)
    ]
    for copy in scalar_copies:
        copy.start()
    def prefetch(i, _):
        for c in range(chunks):
            hid_copy(i, c).start()
        return 0

    lax.fori_loop(0, ahead_rows, prefetch, 0)

    barrier = pltpu.get_barrier_semaphore()
    bits = seq_count.bit_length() - 1
    unrolled = devices <= UNROLLED
    mirrored = unrolled and seq_count == 1 << bits
    flips = [(1 << i) * (1 - 2 * lax.rem(lax.div(me_seq, 1 << i), 2)) for i in range(bits)]

    def peer(k):
        if not mirrored:
            slot = lax.rem(my_slot + k, devices)
            return (lax.rem(slot, seq_count), lax.div(slot, seq_count))
        far, turn = divmod(devices - k, tensor_count)
        seq = me_seq
        for i in range(bits):
            if far >> i & 1:
                seq = seq + flips[i]
        return (seq, lax.rem(me_ten + turn, tensor_count))

    def each_peer(act):
        if unrolled:
            for k in range(1, devices):
                act(k, 0)
        else:
            lax.fori_loop(1, devices, act, 0)

    def greet(k, _):
        pl.semaphore_signal(
            barrier, inc=1, device_id=peer(k), device_id_type=pl.DeviceIdType.MESH
        )
        return 0

    each_peer(greet)

    wait_group(near, near_sem)
    for copy in scalar_copies:
        copy.wait()

    for j in range(local_width // LANES):
        cols = pl.ds(j * LANES, LANES)
        row = gain[cols].astype(jnp.float32) * wgt[cols].astype(jnp.float32)
        scaled[:, cols] = jnp.broadcast_to(row.reshape(1, LANES), (8, LANES))

    lane = lax.broadcasted_iota(jnp.int32, (8, length), 1).astype(jnp.float32)
    after = lax.broadcasted_iota(jnp.int32, (BLOCK, length), 1).astype(jnp.float32)
    before = lax.broadcasted_iota(jnp.int32, (BLOCK, length), 0).astype(jnp.float32)

    def coef_of(last_done, row):
        shape = last_done.shape[:-1] + (length,)
        at = lax.broadcasted_iota(jnp.int32, shape, len(shape) - 1).astype(jnp.float32)
        discount = jnp.full(shape, disc[row], jnp.float32)
        decay = discount * jnp.full(shape, trc[row], jnp.float32)
        power = jnp.exp((length - 1.0 - at) * jnp.log(decay))
        return jnp.where(at > last_done[..., 0:1], discount * power, 0.0)

    rows_info = []
    for r in range(own_rows):
        trace = jnp.full((8, length), trc[first_row + r], jnp.float32)
        decay = jnp.full((BLOCK, length), disc[first_row + r], jnp.float32) * trace[0, 0]
        log_decay = jnp.log(decay)
        flags = jnp.broadcast_to(flg[pl.ds(first_row + r, 1), :], (BLOCK, length)) > 0
        last_done = jnp.max(
            jnp.where(flags[0:8, :], lane, -1.0)[0:1, :], axis=1, keepdims=True
        )
        board[my_slot, r : r + 1, done_lanes] = jnp.broadcast_to(last_done, (1, LANES))
        rows_info.append(dict(trace=trace))
        for b in range(length // BLOCK):
            at = before + float(b * BLOCK)
            gap = after - at
            stop = jnp.where(flags & (gap >= 0.0), after, float(length))
            stop = jnp.min(stop, axis=1, keepdims=True)
            reach[r, pl.ds(b * BLOCK, BLOCK), :] = jnp.where(
                (gap >= 0.0) & (after <= stop), jnp.exp(gap * log_decay), 0.0
            )

    def add_chunk(i, c):
        for b in range(chunk // BLOCK):
            rows = pl.ds(c * chunk + b * BLOCK, BLOCK)
            squares = jnp.zeros((BLOCK // 8, 8, LANES), jnp.float32)
            products = jnp.zeros((BLOCK // 8, 8, LANES), jnp.float32)
            for j in range(local_width // LANES):
                cols = pl.ds(j * LANES, LANES)
                x = hid[i, rows, cols].astype(jnp.float32).reshape(BLOCK // 8, 8, LANES)
                squares = squares + x * x
                products = products + x * scaled[:, cols][None]
            parts[i % 2, 0, rows, :] = squares.reshape(BLOCK, LANES)
            parts[i % 2, 1, rows, :] = products.reshape(BLOCK, LANES)

    part_copies = [
        pltpu.make_async_remote_copy(
            src_ref=part_send.at[k - 1],
            dst_ref=part_recv.at[k - 1],
            send_sem=part_send_sem.at[k - 1],
            recv_sem=part_recv_sem.at[k - 1],
            device_id=(me_seq, lax.rem(me_ten + k, tensor_count)),
            device_id_type=pl.DeviceIdType.MESH,
        )
        for k in range(1, tensor_count)
    ]

    def send_all(lanes, recv_sem):
        def send(k, _):
            pltpu.make_async_remote_copy(
                src_ref=board.at[my_slot, :, lanes],
                dst_ref=board.at[my_slot, :, lanes],
                send_sem=send_sem,
                recv_sem=recv_sem,
                device_id=peer(k),
                device_id_type=pl.DeviceIdType.MESH,
            ).start()
            return 0

        each_peer(send)

    def all_blocks(lanes, sem):
        view = board.at[pl.ds(0, devices - 1), :, lanes]
        return pltpu.make_async_copy(view, view, sem)

    def publish():
        wait_group(far, far_sem)
        for r in range(own_rows):
            ratio = jnp.exp(newp[r : r + 1, :] - oldp[r : r + 1, :])
            weight = msk[r : r + 1, :].astype(jnp.float32)
            reward = jnp.broadcast_to(rew[pl.ds(first_row + r, 1), :], (8, length))
            rows_info[r].update(ratio=ratio, weight=weight, reward=reward)
            board[my_slot, r : r + 1, pl.ds(0, length)] = ratio
            board[my_slot, r : r + 1, weight_lanes] = weight
        send_all(early_lanes, early_recv_sem)

    squares_of = [[] for _ in range(seqs_all)]
    products_of = [[] for _ in range(seqs_all)]
    pending = []

    half = lambda axis: lax.broadcasted_iota(jnp.int32, (16, 2 * LANES), axis)
    pick = jnp.where((half(0) < 8) == (half(1) < LANES), 1.0, 0.0).astype(jnp.bfloat16)

    def flush():
        while pending:
            i, start, stop = pending.pop()
            rows = pl.ds(start, stop - start)
            squares = split(parts[i % 2, 0, rows, :], 3)
            products = split(parts[i % 2, 1, rows, :], 3)
            both = sum(lane_sums(pick, pair) for pair in zip(squares, products))
            squares_of[i].append(both[0:8, :])
            products_of[i].append(both[8:16, :])

    partner_rows = seqs_all - own_rows
    group = length
    for i in range(seqs_all):
        start = 0
        for c in range(chunks):
            hid_copy(i, c).wait()
            if i + ahead_rows < seqs_all:
                hid_copy(i + ahead_rows, c).start()
            if i == partner_rows and c == 1:
                publish()
            flush()
            add_chunk(i, c)
            if i > 0 and c == 0 and i <= partner_rows:
                k, r = divmod(i - 1, own_rows)
                squares = jnp.concatenate(squares_of[i - 1], axis=1)
                products = jnp.concatenate(products_of[i - 1], axis=1)
                part_send[k, 2 * r : 2 * r + 1, :] = squares[0:1, :]
                part_send[k, 2 * r + 1 : 2 * r + 2, :] = products[0:1, :]
            if i == partner_rows and c == 0:
                pl.semaphore_wait(barrier, devices - 1)
                for copy in part_copies:
                    copy.start()
            done = (c + 1) * chunk
            if done % group == 0 or done == length:
                pending.append((i, start, done))
                start = done
    flush()
    for copy in part_copies:
        copy.wait()

    for r in range(own_rows):
        trace, reward = rows_info[r]["trace"], rows_info[r]["reward"]
        squares = jnp.concatenate(squares_of[partner_rows + r], axis=1)
        products = jnp.concatenate(products_of[partner_rows + r], axis=1)
        for k in range(1, tensor_count):
            squares = squares + part_recv[k - 1, 2 * r : 2 * r + 1, :]
            products = products + part_recv[k - 1, 2 * r + 1 : 2 * r + 2, :]
        values = products * lax.rsqrt(squares / width + EPS_NORM)
        values_ref[r : r + 1, :] = values[0:1, :]
        pull = reward + (1.0 - trace) / trace * values
        for b in range(length // 8):
            rows = pl.ds(b * 8, 8)
            terms = reach[r, rows, :] * pull
            parts[0, 0, rows, :] = sum(
                terms[:, n * LANES : (n + 1) * LANES] for n in range(length // LANES)
            )
        ones = jnp.ones((8, LANES), jnp.bfloat16)
        adv = sum(lane_sums(ones, [piece]) for piece in split(parts[0, 0], 3)) - values / trace
        board[my_slot, r : r + 1, adv_lanes] = adv[0:1, :]
        board[my_slot, r : r + 1, offset_lanes] = jnp.broadcast_to(
            values[0:1, 0:1] + trace[0:1, 0:1] * adv[0:1, 0:1], (1, LANES)
        )

    send_all(late_lanes, late_recv_sem)

    all_blocks(early_lanes, early_recv_sem).wait()
    everyone = [
        (t * own_rows + r, pl.ds(t * seq_count, seq_count), r)
        for t in range(tensor_count)
        for r in range(own_rows)
    ]
    total = lambda x: jnp.sum(jnp.sum(x, axis=0, keepdims=True), axis=1, keepdims=True)
    count = jnp.zeros((seq_count, length), jnp.float32)
    coefs = []
    for row, slots, r in everyone:
        count = count + board[slots, r, weight_lanes]
        coef = coef_of(board[slots, r, done_lanes], row)
        coefs.append(coef)
        slope[slots, r, :] = jnp.broadcast_to(trc[row] * coef[:, 0:1], (seq_count, LANES))
    each = 1.0 / total(count)
    own_coefs = [coef_of(board[my_slot, r : r + 1, done_lanes], first_row + r) for r in range(own_rows)]
    all_blocks(late_lanes, late_recv_sem).wait()

    for row, slots, r in everyone:
        entering = jnp.full((1, LANES), boot[row], jnp.float32)
        for n in range(seq_count - 1, -1, -1):
            slot = slots.start + n
            carry[slot, r : r + 1, :] = entering
            if n:
                offset = board[slot, r : r + 1, offset_lanes]
                entering = offset + slope[slot, r : r + 1, :] * entering
    advs = []
    sums = jnp.zeros((seq_count, length), jnp.float32)
    for row, slots, r in everyone:
        entering = jnp.concatenate([carry[slots, r, :]] * (length // LANES), axis=1)
        adv = board[slots, r, adv_lanes] + coefs[row] * entering
        advs.append(adv)
        sums = sums + board[slots, r, weight_lanes] * adv
    mean = total(sums) * each

    def token_loss(ratio, weight, white):
        clipped = jnp.clip(ratio, 1.0 - CLIP, 1.0 + CLIP)
        return -weight * jnp.minimum(ratio * white, clipped * white)

    spread = jnp.zeros((seq_count, length), jnp.float32)
    losses = jnp.zeros((seq_count, length), jnp.float32)
    for row, slots, r in everyone:
        centred = advs[row] - mean
        weight = board[slots, r, weight_lanes]
        spread = spread + weight * centred * centred
        losses = losses + token_loss(board[slots, r, pl.ds(0, length)], weight, centred)
    scale = lax.rsqrt(total(spread) * each + EPS_WHITE)
    loss_ref[...] = jnp.broadcast_to(total(losses) * each * scale, (1, LANES))

    for r in range(own_rows):
        entering = jnp.concatenate([carry[my_slot, r : r + 1, :]] * (length // LANES), axis=1)
        adv = board[my_slot, r : r + 1, adv_lanes] + own_coefs[r] * entering
        white = (adv - mean) * scale
        white_ref[r : r + 1, :] = white
        token_ref[r : r + 1, :] = token_loss(rows_info[r]["ratio"], rows_info[r]["weight"], white)

    view = board.at[pl.ds(0, devices - 1)]
    pltpu.make_async_copy(view, view, send_sem).wait()


def write_out(*refs):
    half = len(refs) // 2
    for src, dst in zip(refs[:half], refs[half:]):
        dst[...] = src[:, : dst.shape[1]]


def shards(seq_count, tensor_count, *args):
    seqs_all, length, local_width = args[0].shape
    own_rows = seqs_all // tensor_count
    devices = seq_count * tensor_count
    chunk = min(length, 64)
    f32 = jnp.float32
    row = jax.ShapeDtypeStruct((own_rows, length), f32)
    dma = pltpu.SemaphoreType.DMA
    others = max(tensor_count - 1, 1)
    shapes = [row, row, row, jax.ShapeDtypeStruct((1, 1), f32)]
    near_bytes = 2 * local_width * 2 + seqs_all * length * 4
    far_bytes = (3 * own_rows + seqs_all) * length * 4
    outs = pl.pallas_call(
        functools.partial(kernel, seq_count, tensor_count, local_width * tensor_count, chunk),
        out_shape=[row, row, row, jax.ShapeDtypeStruct((1, LANES), f32)],
        in_specs=[pl.BlockSpec(memory_space=pltpu.HBM)] * 11,
        out_specs=[pl.BlockSpec(memory_space=pltpu.VMEM)] * 4,
        scratch_shapes=[
            pltpu.VMEM((seqs_all, length, local_width), jnp.bfloat16),
            pltpu.VMEM((local_width,), jnp.bfloat16),
            pltpu.VMEM((local_width,), jnp.bfloat16),
            pltpu.VMEM((seqs_all, length), f32),
            pltpu.VMEM((seqs_all, length), jnp.int32),
            pltpu.VMEM((own_rows, length), jnp.int32),
            pltpu.VMEM((own_rows, length), f32),
            pltpu.VMEM((own_rows, length), f32),
            pltpu.SMEM((seqs_all,), f32),
            pltpu.SMEM((seqs_all,), f32),
            pltpu.SMEM((seqs_all,), f32),
            pltpu.VMEM((max(near_bytes, far_bytes) // (4 * LANES), 1, LANES), f32),
            pltpu.VMEM((8, local_width), f32),
            pltpu.VMEM((2, 2, length, LANES), f32),
            pltpu.VMEM((own_rows, length, length), f32),
            pltpu.VMEM((others, 2 * own_rows, length), f32),
            pltpu.VMEM((others, 2 * own_rows, length), f32),
            pltpu.VMEM((devices, own_rows, 3 * length + 2 * LANES), f32),
            pltpu.VMEM((devices, own_rows, LANES), f32),
            pltpu.VMEM((devices, own_rows, LANES), f32),
            dma((min(seqs_all, AHEAD_ROWS) * (length // chunk),)),
            dma,
            dma,
            dma((3,)),
            dma((others,)),
            dma((others,)),
            dma,
            dma,
            dma,
        ],
        compiler_params=pltpu.CompilerParams(
            collective_id=0, has_side_effects=True, vmem_limit_bytes=24 << 20
        ),
    )(*[pltpu.with_memory_space_constraint(x, pltpu.HBM) for x in args])
    outs = pl.pallas_call(
        write_out,
        out_shape=shapes,
        in_specs=[pl.BlockSpec(memory_space=pltpu.VMEM)] * 4,
        out_specs=[pl.BlockSpec(memory_space=pltpu.VMEM)] * 4,
        compiler_params=pltpu.CompilerParams(vmem_limit_bytes=1 << 20),
    )(*outs)
    return (outs[0], outs[1], outs[2], outs[3].reshape(()))


def solution(mesh):
    in_specs = (
        P(None, "seq", "tensor"),
        P("tensor"),
        P("tensor"),
        P(None, "seq"),
        P(None, "seq"),
        P("tensor", "seq"),
        P("tensor", "seq"),
        P("tensor", "seq"),
        P(),
        P(),
        P(),
    )
    out_specs = (P("tensor", "seq"), P("tensor", "seq"), P("tensor", "seq"), P())
    body = functools.partial(shards, mesh.shape["seq"], mesh.shape["tensor"])
    return jax.shard_map(body, mesh=mesh, in_specs=in_specs, out_specs=out_specs, check_vma=False)
```

time: 14.6 us -> 13.6 us (0.932)
  Pallas kernels: 13.7 us -> 12.8 us
    pallas_call x1, Pallas kernels: 13.1 us -> 12.3 us  [shards(): pl.pallas_call(functools.partial(kernel, seq_count, tensor_count, local_w...]
where the time goes in v1:
time: 13.6 us; the launch traced here: 13.5 us
  Pallas kernels  12.8 us (94%)
  between operations  0.64 us (5%)
    pallas_call x1, Pallas kernels, shards(): pl.pallas_call(functools.partial(kernel, seq_count, tensor_count, local_w...  12.3 us
    pallas_call x1, Pallas kernels, shards(): pl.pallas_call(write_out, out_shape=shapes, in_specs=[pl.BlockSpec(memory...  0.58 us

profile of v1, /device:TPU:0, one launch (start us, length us, event | category | flops | bytes accessed | tf_op | source)
XLA Modules:
  0.0 13.5 jit_solution(1885078628679757935)
XLA Ops:
  0.6 12.3 %shard_map.138 = (f32[1,256]{1,0:T(1,128)S(1)}, f32[1,256]{1,0:T(1,128)S(1)}, f32[1,256]{1,0:T(1,128)S(1)}, f32[1,128]{1,0:T(1,128)S(1)}) custom-call(bf16[2,256,4096]{2,1,0:T(8,128)(2,1)} %hidden_hbm.1, bf16[4096]{0:T(1024)(128)(2,1)} %gain_hbm.1, bf16[4096]{0:T(1024)(128)(2,1)} %weight_hbm.1, f32[2,256]{1,0:T(2,128)} %rewards_hbm.1, s32[2,256]{1,0:T(2,128)} %flags_hbm.1, ...), custom_call_target="tpu_custom_call" | custom-call | tf_op jit(solution)/shard_map/pallas_call | solution.py:411
  12.9 0.6 %shard_map.139 = (f32[1,256]{1,0:T(1,128)}, f32[1,256]{1,0:T(1,128)}, f32[1,256]{1,0:T(1,128)}, f32[1,1]{1,0:T(1,128)}) custom-call(f32[1,256]{1,0:T(1,128)S(1)} %get-tuple-element.12.refs_0_, f32[1,256]{1,0:T(1,128)S(1)} %get-tuple-element.13.refs_1_, f32[1,256]{1,0:T(1,128)S(1)} %get-tuple-element.14.refs_2_, f32[1,128]{1,0:T(1,128)S(1)} %get-tuple-element.15.refs_3_), custom_call_target="tpu_custom_call" | custom-call | tf_op jit(solution)/shard_map/pallas_call | solution.py:451

commit v2 on v1

--- a/solution.py
+++ b/solution.py
@@ -117,19 +117,22 @@
 
     for src, dst in near:
         pltpu.make_async_copy(src, dst, near_sem).start()
-    for src, dst in far:
-        pltpu.make_async_copy(src, dst, far_sem).start()
     scalar_copies = [
         pltpu.make_async_copy(src, dst, scalar_sem.at[i]) for i, (src, dst) in enumerate(scalars)
     ]
-    for copy in scalar_copies:
+    for copy in scalar_copies[0:2]:
         copy.start()
+
     def prefetch(i, _):
         for c in range(chunks):
             hid_copy(i, c).start()
         return 0
 
     lax.fori_loop(0, ahead_rows, prefetch, 0)
+
+    scalar_copies[2].start()
+    for src, dst in far:
+        pltpu.make_async_copy(src, dst, far_sem).start()
 
     barrier = pltpu.get_barrier_semaphore()
     bits = seq_count.bit_length() - 1
@@ -146,7 +149,7 @@
         for i in range(bits):
             if far >> i & 1:
                 seq = seq + flips[i]
-        return (seq, lax.rem(me_ten + turn, tensor_count))
+        return (seq, tensor_count - 1 - turn if far else lax.rem(me_ten + turn, tensor_count))
 
     def each_peer(act):
         if unrolled:
@@ -164,7 +167,7 @@
     each_peer(greet)
 
     wait_group(near, near_sem)
-    for copy in scalar_copies:
+    for copy in scalar_copies[0:2]:
         copy.wait()
 
     for j in range(local_width // LANES):
@@ -249,6 +252,7 @@
 
     def publish():
         wait_group(far, far_sem)
+        scalar_copies[2].wait()
         for r in range(own_rows):
             ratio = jnp.exp(newp[r : r + 1, :] - oldp[r : r + 1, :])
             weight = msk[r : r + 1, :].astype(jnp.float32)
@@ -283,20 +287,20 @@
             hid_copy(i, c).wait()
             if i + ahead_rows < seqs_all:
                 hid_copy(i + ahead_rows, c).start()
-            if i == partner_rows and c == 1:
-                publish()
-            flush()
-            add_chunk(i, c)
-            if i > 0 and c == 0 and i <= partner_rows:
+            if i > 0 and c == 1 and i <= partner_rows:
                 k, r = divmod(i - 1, own_rows)
                 squares = jnp.concatenate(squares_of[i - 1], axis=1)
                 products = jnp.concatenate(products_of[i - 1], axis=1)
                 part_send[k, 2 * r : 2 * r + 1, :] = squares[0:1, :]
                 part_send[k, 2 * r + 1 : 2 * r + 2, :] = products[0:1, :]
-            if i == partner_rows and c == 0:
+            if i == partner_rows and c == 1:
                 pl.semaphore_wait(barrier, devices - 1)
                 for copy in part_copies:
                     copy.start()
+            if i == partner_rows and c == 1:
+                publish()
+            flush()
+            add_chunk(i, c)
             done = (c + 1) * chunk
             if done % group == 0 or done == length:
                 pending.append((i, start, done))
@@ -315,14 +319,13 @@
         values = products * lax.rsqrt(squares / width + EPS_NORM)
         values_ref[r : r + 1, :] = values[0:1, :]
         pull = reward + (1.0 - trace) / trace * values
+        pulled = []
         for b in range(length // 8):
-            rows = pl.ds(b * 8, 8)
-            terms = reach[r, rows, :] * pull
-            parts[0, 0, rows, :] = sum(
-                terms[:, n * LANES : (n + 1) * LANES] for n in range(length // LANES)
-            )
+            terms = reach[r, pl.ds(b * 8, 8), :] * pull
+            pulled.append(sum(terms[:, n * LANES : (n + 1) * LANES] for n in range(length // LANES)))
+        pulled = jnp.concatenate(pulled, axis=0)
         ones = jnp.ones((8, LANES), jnp.bfloat16)
-        adv = sum(lane_sums(ones, [piece]) for piece in split(parts[0, 0], 3)) - values / trace
+        adv = sum(lane_sums(ones, [piece]) for piece in split(pulled, 3)) - values / trace
         board[my_slot, r : r + 1, adv_lanes] = adv[0:1, :]
         board[my_slot, r : r + 1, offset_lanes] = jnp.broadcast_to(
             values[0:1, 0:1] + trace[0:1, 0:1] * adv[0:1, 0:1], (1, LANES)

time: 13.6 us -> 13.6 us (level)
  no operation moved by 1% of the time
where the time goes in v2:
time: 13.6 us; the launch traced here: 13.4 us
  Pallas kernels  12.8 us (94%)
  between operations  0.64 us (5%)
    pallas_call x1, Pallas kernels, shards(): pl.pallas_call(functools.partial(kernel, seq_count, tensor_count, local_w...  12.2 us
    pallas_call x1, Pallas kernels, shards(): pl.pallas_call(write_out, out_shape=shapes, in_specs=[pl.BlockSpec(memory...  0.58 us

profile of v2, /device:TPU:0, one launch (start us, length us, event | category | flops | bytes accessed | tf_op | source)
XLA Modules:
  0.0 13.4 jit_solution(14955635771706701639)
XLA Ops:
  0.6 12.2 %shard_map.138 = (f32[1,256]{1,0:T(1,128)S(1)}, f32[1,256]{1,0:T(1,128)S(1)}, f32[1,256]{1,0:T(1,128)S(1)}, f32[1,128]{1,0:T(1,128)S(1)}) custom-call(bf16[2,256,4096]{2,1,0:T(8,128)(2,1)} %hidden_hbm.1, bf16[4096]{0:T(1024)(128)(2,1)} %gain_hbm.1, bf16[4096]{0:T(1024)(128)(2,1)} %weight_hbm.1, f32[2,256]{1,0:T(2,128)} %rewards_hbm.1, s32[2,256]{1,0:T(2,128)} %flags_hbm.1, ...), custom_call_target="tpu_custom_call" | custom-call | tf_op jit(solution)/shard_map/pallas_call | solution.py:414
  12.9 0.6 %shard_map.139 = (f32[1,256]{1,0:T(1,128)}, f32[1,256]{1,0:T(1,128)}, f32[1,256]{1,0:T(1,128)}, f32[1,1]{1,0:T(1,128)}) custom-call(f32[1,256]{1,0:T(1,128)S(1)} %get-tuple-element.12.refs_0_, f32[1,256]{1,0:T(1,128)S(1)} %get-tuple-element.13.refs_1_, f32[1,256]{1,0:T(1,128)S(1)} %get-tuple-element.14.refs_2_, f32[1,128]{1,0:T(1,128)S(1)} %get-tuple-element.15.refs_3_), custom_call_target="tpu_custom_call" | custom-call | tf_op jit(solution)/shard_map/pallas_call | solution.py:454

commit v3 on v2

--- a/solution.py
+++ b/solution.py
@@ -13,6 +13,7 @@
 LANES = 128
 BLOCK = 32
 UNROLLED = 64
+PIECES = 3
 AHEAD_ROWS = 2
 
 
@@ -81,6 +82,7 @@
     part_recv_sem,
     send_sem,
     early_recv_sem,
+    forward_recv_sem,
     late_recv_sem,
 ):
     seqs_all, length, local_width = hid.shape
@@ -200,12 +202,11 @@
         rows_info.append(dict(trace=trace))
         for b in range(length // BLOCK):
             at = before + float(b * BLOCK)
-            gap = after - at
-            stop = jnp.where(flags & (gap >= 0.0), after, float(length))
-            stop = jnp.min(stop, axis=1, keepdims=True)
-            reach[r, pl.ds(b * BLOCK, BLOCK), :] = jnp.where(
-                (gap >= 0.0) & (after <= stop), jnp.exp(gap * log_decay), 0.0
-            )
+            gap = at - after
+            last = jnp.max(jnp.where(flags & (gap > 0.0), after, -1.0), axis=1, keepdims=True)
+            block = jnp.where((gap >= 0.0) & (after > last), jnp.exp(gap * log_decay), 0.0)
+            for n, piece in enumerate(split(block, PIECES)):
+                reach[n, r, pl.ds(b * BLOCK, BLOCK), :] = piece
 
     def add_chunk(i, c):
         for b in range(chunk // BLOCK):
@@ -232,6 +233,43 @@
         for k in range(1, tensor_count)
     ]
 
+    def send_column():
+        def send(k, _):
+            if mirrored:
+                seq = me_seq
+                for i in range(bits):
+                    if (seq_count - k) >> i & 1:
+                        seq = seq + flips[i]
+            else:
+                seq = lax.rem(me_seq + k, seq_count)
+            pltpu.make_async_remote_copy(
+                src_ref=board.at[my_slot, :, early_lanes],
+                dst_ref=board.at[my_slot, :, early_lanes],
+                send_sem=send_sem,
+                recv_sem=early_recv_sem,
+                device_id=(seq, me_ten),
+                device_id_type=pl.DeviceIdType.MESH,
+            ).start()
+            return 0
+
+        if unrolled:
+            for k in range(1, seq_count):
+                send(k, 0)
+        else:
+            lax.fori_loop(1, seq_count, send, 0)
+
+    def forward_column():
+        column = board.at[pl.ds(me_ten * seq_count, seq_count), :, early_lanes]
+        for k in range(1, tensor_count):
+            pltpu.make_async_remote_copy(
+                src_ref=column,
+                dst_ref=column,
+                send_sem=send_sem,
+                recv_sem=forward_recv_sem,
+                device_id=(me_seq, lax.rem(me_ten + k, tensor_count)),
+                device_id_type=pl.DeviceIdType.MESH,
+            ).start()
+
     def send_all(lanes, recv_sem):
         def send(k, _):
             pltpu.make_async_remote_copy(
@@ -246,8 +284,8 @@
 
         each_peer(send)
 
-    def all_blocks(lanes, sem):
-        view = board.at[pl.ds(0, devices - 1), :, lanes]
+    def blocks(count, lanes, sem):
+        view = board.at[pl.ds(0, count), :, lanes]
         return pltpu.make_async_copy(view, view, sem)
 
     def publish():
@@ -260,7 +298,7 @@
             rows_info[r].update(ratio=ratio, weight=weight, reward=reward)
             board[my_slot, r : r + 1, pl.ds(0, length)] = ratio
             board[my_slot, r : r + 1, weight_lanes] = weight
-        send_all(early_lanes, early_recv_sem)
+        send_column()
 
     squares_of = [[] for _ in range(seqs_all)]
     products_of = [[] for _ in range(seqs_all)]
@@ -273,9 +311,10 @@
         while pending:
             i, start, stop = pending.pop()
             rows = pl.ds(start, stop - start)
-            squares = split(parts[i % 2, 0, rows, :], 3)
+            squares = split(parts[i % 2, 0, rows, :], 2)
             products = split(parts[i % 2, 1, rows, :], 3)
             both = sum(lane_sums(pick, pair) for pair in zip(squares, products))
+            both = both + lane_sums(pick[:, LANES:], products[2:])
             squares_of[i].append(both[0:8, :])
             products_of[i].append(both[8:16, :])
 
@@ -319,13 +358,22 @@
         values = products * lax.rsqrt(squares / width + EPS_NORM)
         values_ref[r : r + 1, :] = values[0:1, :]
         pull = reward + (1.0 - trace) / trace * values
-        pulled = []
-        for b in range(length // 8):
-            terms = reach[r, pl.ds(b * 8, 8), :] * pull
-            pulled.append(sum(terms[:, n * LANES : (n + 1) * LANES] for n in range(length // LANES)))
-        pulled = jnp.concatenate(pulled, axis=0)
-        ones = jnp.ones((8, LANES), jnp.bfloat16)
-        adv = sum(lane_sums(ones, [piece]) for piece in split(pulled, 3)) - values / trace
+        rest, rows = pull, []
+        for _ in range(PIECES):
+            rows.append(rest.astype(jnp.bfloat16).astype(jnp.float32))
+            rest = rest - rows[-1]
+        rows = jnp.concatenate(rows + [rest], axis=0).astype(jnp.bfloat16)
+        adv = -values / trace
+        for n in range(PIECES):
+            used = PIECES - n
+            summed = lax.dot_general(
+                rows[0 : 16 * pl.cdiv(used, 2), :],
+                reach[n, r],
+                (((1,), (0,)), ((), ())),
+                preferred_element_type=jnp.float32,
+            )
+            for m in range(used):
+                adv = adv + summed[8 * m : 8 * m + 8, :]
         board[my_slot, r : r + 1, adv_lanes] = adv[0:1, :]
         board[my_slot, r : r + 1, offset_lanes] = jnp.broadcast_to(
             values[0:1, 0:1] + trace[0:1, 0:1] * adv[0:1, 0:1], (1, LANES)
@@ -333,7 +381,9 @@
 
     send_all(late_lanes, late_recv_sem)
 
-    all_blocks(early_lanes, early_recv_sem).wait()
+    blocks(seq_count - 1, early_lanes, early_recv_sem).wait()
+    forward_column()
+    blocks(devices - seq_count, early_lanes, forward_recv_sem).wait()
     everyone = [
         (t * own_rows + r, pl.ds(t * seq_count, seq_count), r)
         for t in range(tensor_count)
@@ -349,7 +399,7 @@
         slope[slots, r, :] = jnp.broadcast_to(trc[row] * coef[:, 0:1], (seq_count, LANES))
     each = 1.0 / total(count)
     own_coefs = [coef_of(board[my_slot, r : r + 1, done_lanes], first_row + r) for r in range(own_rows)]
-    all_blocks(late_lanes, late_recv_sem).wait()
+    blocks(devices - 1, late_lanes, late_recv_sem).wait()
 
     for row, slots, r in everyone:
         entering = jnp.full((1, LANES), boot[row], jnp.float32)
@@ -431,7 +481,7 @@
             pltpu.VMEM((max(near_bytes, far_bytes) // (4 * LANES), 1, LANES), f32),
             pltpu.VMEM((8, local_width), f32),
             pltpu.VMEM((2, 2, length, LANES), f32),
-            pltpu.VMEM((own_rows, length, length), f32),
+            pltpu.VMEM((PIECES, own_rows, length, length), jnp.bfloat16),
             pltpu.VMEM((others, 2 * own_rows, length), f32),
             pltpu.VMEM((others, 2 * own_rows, length), f32),
             pltpu.VMEM((devices, own_rows, 3 * length + 2 * LANES), f32),
@@ -443,6 +493,7 @@
             dma((3,)),
             dma((others,)),
             dma((others,)),
+            dma,
             dma,
             dma,
             dma,

time: 13.6 us -> 13.5 us (level)
  no operation moved by 1% of the time
where the time goes in v3:
time: 13.5 us; the launch traced here: 13.3 us
  Pallas kernels  12.7 us (94%)
  between operations  0.64 us (5%)
    pallas_call x1, Pallas kernels, shards(): pl.pallas_call(functools.partial(kernel, seq_count, tensor_count, local_w...  12.1 us
    pallas_call x1, Pallas kernels, shards(): pl.pallas_call(write_out, out_shape=shapes, in_specs=[pl.BlockSpec(memory...  0.58 us

profile of v3, /device:TPU:0, one launch (start us, length us, event | category | flops | bytes accessed | tf_op | source)
XLA Modules:
  0.0 13.3 jit_solution(12058202717880305954)
XLA Ops:
  0.6 12.1 %shard_map.138 = (f32[1,256]{1,0:T(1,128)S(1)}, f32[1,256]{1,0:T(1,128)S(1)}, f32[1,256]{1,0:T(1,128)S(1)}, f32[1,128]{1,0:T(1,128)S(1)}) custom-call(bf16[2,256,4096]{2,1,0:T(8,128)(2,1)} %hidden_hbm.1, bf16[4096]{0:T(1024)(128)(2,1)} %gain_hbm.1, bf16[4096]{0:T(1024)(128)(2,1)} %weight_hbm.1, f32[2,256]{1,0:T(2,128)} %rewards_hbm.1, s32[2,256]{1,0:T(2,128)} %flags_hbm.1, ...), custom_call_target="tpu_custom_call" | custom-call | tf_op jit(solution)/shard_map/pallas_call | solution.py:464
  12.8 0.6 %shard_map.139 = (f32[1,256]{1,0:T(1,128)}, f32[1,256]{1,0:T(1,128)}, f32[1,256]{1,0:T(1,128)}, f32[1,1]{1,0:T(1,128)}) custom-call(f32[1,256]{1,0:T(1,128)S(1)} %get-tuple-element.12.refs_0_, f32[1,256]{1,0:T(1,128)S(1)} %get-tuple-element.13.refs_1_, f32[1,256]{1,0:T(1,128)S(1)} %get-tuple-element.14.refs_2_, f32[1,128]{1,0:T(1,128)S(1)} %get-tuple-element.15.refs_3_), custom_call_target="tpu_custom_call" | custom-call | tf_op jit(solution)/shard_map/pallas_call | solution.py:505

commit v4 on v3

--- a/solution.py
+++ b/solution.py
@@ -309,7 +309,7 @@
 
     def flush():
         while pending:
-            i, start, stop = pending.pop()
+            i, start, stop = pending.pop(0)
             rows = pl.ds(start, stop - start)
             squares = split(parts[i % 2, 0, rows, :], 2)
             products = split(parts[i % 2, 1, rows, :], 3)
@@ -319,7 +319,6 @@
             products_of[i].append(both[8:16, :])
 
     partner_rows = seqs_all - own_rows
-    group = length
     for i in range(seqs_all):
         start = 0
         for c in range(chunks):
@@ -338,10 +337,11 @@
                     copy.start()
             if i == partner_rows and c == 1:
                 publish()
-            flush()
+            if i < partner_rows or c in (0, chunks - 1):
+                flush()
             add_chunk(i, c)
             done = (c + 1) * chunk
-            if done % group == 0 or done == length:
+            if done == length or i >= partner_rows and done % LANES == 0:
                 pending.append((i, start, done))
                 start = done
     flush()
@@ -390,32 +390,42 @@
         for r in range(own_rows)
     ]
     total = lambda x: jnp.sum(jnp.sum(x, axis=0, keepdims=True), axis=1, keepdims=True)
+    def gather(slots, r, start):
+        return jnp.concatenate(
+            [board[slots, r, pl.ds(start + n, LANES)] for n in range(0, length, LANES)], axis=1
+        )
+
     count = jnp.zeros((seq_count, length), jnp.float32)
-    coefs = []
+    coefs, chains = [], []
+    place = lax.broadcasted_iota(jnp.int32, (seq_count, LANES), 0)
     for row, slots, r in everyone:
-        count = count + board[slots, r, weight_lanes]
+        count = count + gather(slots, r, length)
         coef = coef_of(board[slots, r, done_lanes], row)
         coefs.append(coef)
         slope[slots, r, :] = jnp.broadcast_to(trc[row] * coef[:, 0:1], (seq_count, LANES))
+        chain = [jnp.where(place == 0, 1.0, 0.0)]
+        for n in range(1, seq_count):
+            step = slope[slots.start + n, r : r + 1, :]
+            chain.append(jnp.where(place == n, 1.0, chain[-1] * step))
+        chains.append(chain)
     each = 1.0 / total(count)
     own_coefs = [coef_of(board[my_slot, r : r + 1, done_lanes], first_row + r) for r in range(own_rows)]
     blocks(devices - 1, late_lanes, late_recv_sem).wait()
 
-    for row, slots, r in everyone:
-        entering = jnp.full((1, LANES), boot[row], jnp.float32)
-        for n in range(seq_count - 1, -1, -1):
-            slot = slots.start + n
-            carry[slot, r : r + 1, :] = entering
-            if n:
-                offset = board[slot, r : r + 1, offset_lanes]
-                entering = offset + slope[slot, r : r + 1, :] * entering
     advs = []
     sums = jnp.zeros((seq_count, length), jnp.float32)
     for row, slots, r in everyone:
-        entering = jnp.concatenate([carry[slots, r, :]] * (length // LANES), axis=1)
-        adv = board[slots, r, adv_lanes] + coefs[row] * entering
+        terms = [boot[row] * chains[row][-1]]
+        for n in range(1, seq_count):
+            offset = board[slots.start + n, r : r + 1, offset_lanes]
+            terms.append(chains[row][n - 1] * offset)
+        while len(terms) > 1:
+            terms = [sum(terms[n : n + 2]) for n in range(0, len(terms), 2)]
+        carry[slots, r, :] = terms[0]
+        entering = jnp.concatenate(terms * (length // LANES), axis=1)
+        adv = gather(slots, r, adv_lanes.start) + coefs[row] * entering
         advs.append(adv)
-        sums = sums + board[slots, r, weight_lanes] * adv
+        sums = sums + gather(slots, r, length) * adv
     mean = total(sums) * each
 
     def token_loss(ratio, weight, white):
@@ -426,9 +436,9 @@
     losses = jnp.zeros((seq_count, length), jnp.float32)
     for row, slots, r in everyone:
         centred = advs[row] - mean
-        weight = board[slots, r, weight_lanes]
+        weight = gather(slots, r, length)
         spread = spread + weight * centred * centred
-        losses = losses + token_loss(board[slots, r, pl.ds(0, length)], weight, centred)
+        losses = losses + token_loss(gather(slots, r, 0), weight, centred)
     scale = lax.rsqrt(total(spread) * each + EPS_WHITE)
     loss_ref[...] = jnp.broadcast_to(total(losses) * each * scale, (1, LANES))
 

time: 13.5 us -> 13.5 us (level)
  no operation moved by 1% of the time
where the time goes in v4:
time: 13.5 us; the launch traced here: 13.3 us
  Pallas kernels  12.7 us (94%)
  between operations  0.64 us (5%)
    pallas_call x1, Pallas kernels, shards(): pl.pallas_call(functools.partial(kernel, seq_count, tensor_count, local_w...  12.1 us
    pallas_call x1, Pallas kernels, shards(): pl.pallas_call(write_out, out_shape=shapes, in_specs=[pl.BlockSpec(memory...  0.58 us

profile of v4, /device:TPU:0, one launch (start us, length us, event | category | flops | bytes accessed | tf_op | source)
XLA Modules:
  0.0 13.3 jit_solution(16864088649222141841)
XLA Ops:
  0.6 12.1 %shard_map.138 = (f32[1,256]{1,0:T(1,128)S(1)}, f32[1,256]{1,0:T(1,128)S(1)}, f32[1,256]{1,0:T(1,128)S(1)}, f32[1,128]{1,0:T(1,128)S(1)}) custom-call(bf16[2,256,4096]{2,1,0:T(8,128)(2,1)} %hidden_hbm.1, bf16[4096]{0:T(1024)(128)(2,1)} %gain_hbm.1, bf16[4096]{0:T(1024)(128)(2,1)} %weight_hbm.1, f32[2,256]{1,0:T(2,128)} %rewards_hbm.1, s32[2,256]{1,0:T(2,128)} %flags_hbm.1, ...), custom_call_target="tpu_custom_call" | custom-call | tf_op jit(solution)/shard_map/pallas_call | solution.py:474
  12.7 0.6 %shard_map.139 = (f32[1,256]{1,0:T(1,128)}, f32[1,256]{1,0:T(1,128)}, f32[1,256]{1,0:T(1,128)}, f32[1,1]{1,0:T(1,128)}) custom-call(f32[1,256]{1,0:T(1,128)S(1)} %get-tuple-element.12.refs_0_, f32[1,256]{1,0:T(1,128)S(1)} %get-tuple-element.13.refs_1_, f32[1,256]{1,0:T(1,128)S(1)} %get-tuple-element.14.refs_2_, f32[1,128]{1,0:T(1,128)S(1)} %get-tuple-element.15.refs_3_), custom_call_target="tpu_custom_call" | custom-call | tf_op jit(solution)/shard_map/pallas_call | solution.py:515

commit v5 on v4

--- a/solution.py
+++ b/solution.py
@@ -78,7 +78,6 @@
     near_sem,
     far_sem,
     scalar_sem,
-    part_send_sem,
     part_recv_sem,
     send_sem,
     early_recv_sem,
@@ -120,7 +119,7 @@
     for src, dst in near:
         pltpu.make_async_copy(src, dst, near_sem).start()
     scalar_copies = [
-        pltpu.make_async_copy(src, dst, scalar_sem.at[i]) for i, (src, dst) in enumerate(scalars)
+        pltpu.make_async_copy(src, dst, scalar_sem.at[i % 2]) for i, (src, dst) in enumerate(scalars)
     ]
     for copy in scalar_copies[0:2]:
         copy.start()
@@ -132,7 +131,6 @@
 
     lax.fori_loop(0, ahead_rows, prefetch, 0)
 
-    scalar_copies[2].start()
     for src, dst in far:
         pltpu.make_async_copy(src, dst, far_sem).start()
 
@@ -171,6 +169,7 @@
     wait_group(near, near_sem)
     for copy in scalar_copies[0:2]:
         copy.wait()
+    scalar_copies[2].start()
 
     for j in range(local_width // LANES):
         cols = pl.ds(j * LANES, LANES)
@@ -225,7 +224,7 @@
         pltpu.make_async_remote_copy(
             src_ref=part_send.at[k - 1],
             dst_ref=part_recv.at[k - 1],
-            send_sem=part_send_sem.at[k - 1],
+            send_sem=near_sem,
             recv_sem=part_recv_sem.at[k - 1],
             device_id=(me_seq, lax.rem(me_ten + k, tensor_count)),
             device_id_type=pl.DeviceIdType.MESH,
@@ -346,7 +345,9 @@
                 start = done
     flush()
     for copy in part_copies:
-        copy.wait()
+        copy.wait_recv()
+    if part_copies:
+        pltpu.make_async_copy(part_send, part_send, near_sem).wait()
 
     for r in range(own_rows):
         trace, reward = rows_info[r]["trace"], rows_info[r]["reward"]
@@ -500,8 +501,7 @@
             dma((min(seqs_all, AHEAD_ROWS) * (length // chunk),)),
             dma,
             dma,
-            dma((3,)),
-            dma((others,)),
+            dma((2,)),
             dma((others,)),
             dma,
             dma,

time: 13.5 us -> 13.5 us (level)
  no operation moved by 1% of the time
where the time goes in v5:
time: 13.5 us; the launch traced here: 13.3 us
  Pallas kernels  12.6 us (93%)
  between operations  0.64 us (5%)
    pallas_call x1, Pallas kernels, shards(): pl.pallas_call(functools.partial(kernel, seq_count, tensor_count, local_w...  12 us
    pallas_call x1, Pallas kernels, shards(): pl.pallas_call(write_out, out_shape=shapes, in_specs=[pl.BlockSpec(memory...  0.58 us

profile of v5, /device:TPU:0, one launch (start us, length us, event | category | flops | bytes accessed | tf_op | source)
XLA Modules:
  0.0 13.3 jit_solution(2653911365940366547)
XLA Ops:
  0.6 12.0 %shard_map.138 = (f32[1,256]{1,0:T(1,128)S(1)}, f32[1,256]{1,0:T(1,128)S(1)}, f32[1,256]{1,0:T(1,128)S(1)}, f32[1,128]{1,0:T(1,128)S(1)}) custom-call(bf16[2,256,4096]{2,1,0:T(8,128)(2,1)} %hidden_hbm.1, bf16[4096]{0:T(1024)(128)(2,1)} %gain_hbm.1, bf16[4096]{0:T(1024)(128)(2,1)} %weight_hbm.1, f32[2,256]{1,0:T(2,128)} %rewards_hbm.1, s32[2,256]{1,0:T(2,128)} %flags_hbm.1, ...), custom_call_target="tpu_custom_call" | custom-call | tf_op jit(solution)/shard_map/pallas_call | solution.py:475
  12.7 0.6 %shard_map.139 = (f32[1,256]{1,0:T(1,128)}, f32[1,256]{1,0:T(1,128)}, f32[1,256]{1,0:T(1,128)}, f32[1,1]{1,0:T(1,128)}) custom-call(f32[1,256]{1,0:T(1,128)S(1)} %get-tuple-element.12.refs_0_, f32[1,256]{1,0:T(1,128)S(1)} %get-tuple-element.13.refs_1_, f32[1,256]{1,0:T(1,128)S(1)} %get-tuple-element.14.refs_2_, f32[1,128]{1,0:T(1,128)S(1)} %get-tuple-element.15.refs_3_), custom_call_target="tpu_custom_call" | custom-call | tf_op jit(solution)/shard_map/pallas_call | solution.py:515
